TPU v7x, 32 devices: a whole 2x2x4 slice. The times are simulated.
32 devices in a mesh: ctx: 16 (over z, x, core), head: 2 (over y).
Axes of the slice: x: 2, y: 2, z: 4, core: 2. Of those that a mesh axis runs over, the one named last changes fastest.
Arguments:
- queries: bfloat16 [2048, 2048], P('ctx', 'head'), may hold values from -160 to 160
- rotated_keys: bfloat16 [2048, 512], P('ctx', 'head'), may hold values from -6 to 6
- value_matrix: bfloat16 [2048, 512], P('ctx', 'head'), may hold values from -6 to 6
- doc_lengths: int32 [8], replicated, may hold values from 1 to 1536, 2048 in all
- scored: int32 [64], P('ctx'), may hold values from 0 to 127, as said below
- residual: bfloat16 [64, 4096], P('ctx', 'head'), may hold values from -18 to 18
- norm_gain: float32 [4096], P('head'), may hold values from 0.5 to 1.5
- out_weight: bfloat16 [2048, 4096], P('head'), may hold values from -0.5 to 0.5
- lm_weight: bfloat16 [4096, 128256], P('head', 'ctx'), may hold values from -0.40625 to 0.40625
- token_ids: int32 [64], replicated, may hold values from 0 to 128255
- old_logp: float32 [64], replicated, may hold values from -24 to -9
- advantage: float32 [64], replicated, may hold values from -3 to 3
Outputs:
- attended: bfloat16 [2048, 2048], P('ctx', 'head')
- log_probs: float32 [64], replicated
- token_loss: float32 [64], replicated
Inputs may be any that keep to these rules, and one draw needn't show every extreme that they name: `scored`: each aligned block of 4 entries holds distinct increasing offsets. `doc_lengths`: the longest document has exactly three quarters of 2048 positions.
All inputs are finite; a program needn't handle non-finite values.
Results may differ from a plain program's by a relative error of at most 0.0065.
Values may be sent and summed in bfloat16 or wider, within the bound.
A program may use at most 128 MiB of HBM per device.

v0:
```python
import math

import jax
import jax.numpy as jnp
from jax import lax
from jax.sharding import PartitionSpec as P

HEAD_SIZE = 128


masked_score = -1e30


def combined_all(value, axis, join):
    pieces = jax.tree.map(lambda part: lax.all_gather(part, axis), value)
    head = jax.tree.map(lambda part: part[0], pieces)
    tail = jax.tree.map(lambda part: part[1:], pieces)
    total, _ = lax.scan(lambda total, slab: (join(total, slab), None), head, tail)
    return total


def doc_index(positions, doc_ends):
    return jnp.sum((positions[:, None] >= doc_ends[None, :]).astype(jnp.int32), axis=1)


def attend_rows(running, context, key_part, value_part, offset):
    query_heads, query_pos, query_doc, doc_ends, first_start, skipping = context
    row_top, row_total, accumulated = running
    row_count = key_part.shape[0]
    kv_heads = query_heads.shape[1]
    key_head_rows = key_part.reshape(row_count, kv_heads, HEAD_SIZE)
    value_head_rows = value_part.reshape(row_count, kv_heads, HEAD_SIZE)
    scores = jnp.einsum(
        "qkgd,rkd->kgqr", query_heads, key_head_rows, preferred_element_type=jnp.float32
    ) * HEAD_SIZE ** (-0.5)
    key_pos = offset + jnp.arange(row_count, dtype=jnp.int32)
    allowed = (
        (key_pos[None, :] <= query_pos[:, None])
        & (key_pos[None, :] >= 0)
        & (doc_index(key_pos, doc_ends)[None, :] == query_doc[:, None])
    )
    scores = jnp.where(allowed, scores, masked_score)
    new_top = jnp.maximum(row_top, jnp.max(scores, axis=-1))
    weights = jnp.where(allowed, jnp.exp(scores - new_top[..., None]), 0.0)
    rescale = jnp.exp(row_top - new_top)
    row_total = row_total * rescale + jnp.sum(weights, axis=-1)
    update = jnp.einsum(
        "kgqr,rkd->kgqd",
        weights.astype(jnp.bfloat16),
        value_head_rows,
        preferred_element_type=jnp.float32,
    )
    accumulated = accumulated * rescale[..., None] + update
    return (new_top, row_total, accumulated)


def attend_piece(running, shard_piece, context):
    key_rows, value_rows = shard_piece
    row_count = key_rows.shape[0]
    block_rows = math.gcd(row_count, 512)
    block_count = row_count // block_rows

    def one_block(block_index, carried):
        start_row = block_index * block_rows
        key_part = lax.dynamic_slice_in_dim(key_rows, start_row, block_rows, 0)
        value_part = lax.dynamic_slice_in_dim(value_rows, start_row, block_rows, 0)
        return attend_rows(carried, context, key_part, value_part, start_row)

    return lax.fori_loop(0, block_count, one_block, running)


def combine(earlier, later):
    top_one, sum_one, target_one = earlier
    top_two, sum_two, target_two = later
    new_top = jnp.maximum(top_one, top_two)
    merged_sum = sum_one * jnp.exp(top_one - new_top) + sum_two * jnp.exp(top_two - new_top)
    return (new_top, merged_sum, target_one + target_two)


def per_device(
    queries,
    rotated_keys,
    value_matrix,
    doc_lengths,
    scored,
    residual,
    norm_gain,
    out_weight,
    lm_weight,
    token_ids,
    old_logp,
    advantage,
):
    tok_rows = queries.shape[0]
    kv_heads = rotated_keys.shape[1] // HEAD_SIZE
    group_count = queries.shape[1] // rotated_keys.shape[1]
    my_index = lax.axis_index("ctx")
    doc_ends = jnp.cumsum(doc_lengths)
    doc_starts = doc_ends - doc_lengths
    query_pos = my_index * tok_rows + jnp.arange(tok_rows, dtype=jnp.int32)
    query_doc = doc_index(query_pos, doc_ends)
    first_start = jnp.max(jnp.where(doc_starts <= query_pos[0], doc_starts, 0))
    query_heads = queries.reshape(tok_rows, kv_heads, group_count, HEAD_SIZE)
    context = (query_heads, query_pos, query_doc, doc_ends, first_start, False)
    state_shape = (kv_heads, group_count, tok_rows)
    initial = (
        jnp.full(state_shape, masked_score, jnp.float32),
        jnp.zeros(state_shape, jnp.float32),
        jnp.zeros(state_shape + (HEAD_SIZE,), jnp.float32),
    )
    row_top, row_total, accumulated = attend_piece(
        initial,
        (
            lax.all_gather(rotated_keys, "ctx", axis=0, tiled=True),
            lax.all_gather(value_matrix, "ctx", axis=0, tiled=True),
        ),
        context,
    )
    result = accumulated / row_total[..., None]
    attended = (
        jnp.transpose(result, (2, 0, 1, 3))
        .reshape(tok_rows, kv_heads * group_count * HEAD_SIZE)
        .astype(jnp.bfloat16)
    )
    chosen = jnp.take(attended, scored, axis=0)
    partial_value = jnp.dot(chosen, out_weight, preferred_element_type=jnp.float32)
    projected = lax.psum_scatter(
        partial_value.astype(jnp.bfloat16), "head", scatter_dimension=1, tiled=True
    ).astype(jnp.float32)
    hidden = residual.astype(jnp.float32) + projected
    squares = lax.psum(jnp.sum(hidden * hidden, axis=1), "head")
    full_width = hidden.shape[1] * lax.axis_size("head")
    normed = (
        hidden * lax.rsqrt(squares[:, None] / full_width + 1e-05) * norm_gain[None, :]
    ).astype(jnp.bfloat16)
    partial_logits = jnp.dot(
        lax.all_gather(normed, "ctx", axis=0, tiled=True),
        lm_weight,
        preferred_element_type=jnp.float32,
    )
    logits = lax.psum_scatter(
        partial_logits.astype(jnp.bfloat16), "head", scatter_dimension=1, tiled=True
    ).astype(jnp.float32)
    vocab_rows = logits.shape[1]
    vocab_start = (
        my_index * vocab_rows * lax.axis_size("head") + lax.axis_index("head") * vocab_rows
    )
    local_ids = token_ids - vocab_start
    matches = local_ids[:, None] == jnp.arange(vocab_rows, dtype=jnp.int32)[None, :]
    target_part = jnp.sum(jnp.where(matches, logits, 0.0), axis=1)
    local_top = jnp.max(logits, axis=1)
    sum_part = jnp.sum(jnp.exp(logits - local_top[:, None]), axis=1)
    global_top, exp_total, target = combined_all(
        (local_top, sum_part, target_part), ("ctx", "head"), combine
    )
    log_probs = target - global_top - jnp.log(exp_total)
    ratio = jnp.exp(jnp.clip(log_probs - old_logp, -4.0, 4.0))
    token_loss = -jnp.minimum(ratio * advantage, jnp.clip(ratio, 0.8, 1.2) * advantage)
    return (attended, log_probs, token_loss)


def solution(mesh):
    return jax.shard_map(
        per_device,
        mesh=mesh,
        in_specs=(
            P("ctx", "head"),
            P("ctx", "head"),
            P("ctx", "head"),
            P(),
            P("ctx"),
            P("ctx", "head"),
            P("head"),
            P("head", None),
            P("head", "ctx"),
            P(),
            P(),
            P(),
        ),
        out_specs=(P("ctx", "head"), P(), P()),
        check_vma=False,
    )
```

profile of v0, /device:TPU:0, one launch (start us, length us, event | category | flops | bytes accessed | tf_op | source)
XLA Modules:
  0.0 262.7 jit_solution(8735908538229840253)
XLA Ops:
  7.2 1.6 copy.36
  8.9 1.6 copy.38
  10.5 0.8 reduce-window.8
  11.4 1.1 copy.37
  12.5 0.2 copy.39
  12.7 0.7 compare_select_fusion
  13.4 0.1 convert_reduce_fusion.1
  13.4 0.7 compare_and_fusion.1
  14.1 36.0 %all-gather.7.cloned.1.call-done = bf16[2048,256]{0,1:T(8,128)(2,1)} async-done(((bf16[128,256]{0,1:T(8,128)(2,1)}), bf16[2048,256]{0,1:T(8,128)(2,1)}) %all-gather.7.cloned.1.call-update) | async-done | bytes 1048592 | tf_op jit(solution)/shard_map/all_gather | solution.py:114
  50.1 38.4 %all-gather.9.cloned.1.call-done = bf16[2048,256]{0,1:T(8,128)(2,1)} async-done(((bf16[128,256]{0,1:T(8,128)(2,1)}), bf16[2048,256]{0,1:T(8,128)(2,1)}) %all-gather.9.cloned.1.call-update) | async-done | bytes 1048592 | tf_op jit(solution)/shard_map/all_gather | solution.py:115
  88.5 14.2 %while.33 = (s32[]{:T(128)}, f32[2,4,128]{2,1,0:T(4,128)S(1)}, f32[2,4,128]{2,1,0:T(4,128)S(1)}, f32[2,4,128,128]{3,2,1,0:T(8,128)S(1)}, s32[8]{0:T(128)S(1)}, /...) while((s32[]{:T(128)}, f32[2,4,128]{2,1,0:T(4,128)S(1)}, ...), condition=%wide.region_6.7_spmd.clone, body=%wide.region_2.6_spmd.clone.sunk | while | flops 275925120 | bytes 9515759 | solution.py:69
  88.5 0.1 convert_reduce_fusion.3
  88.7 0.3 compare_and_fusion.3
  88.9 1.1 constant_dynamic-slice_fusion.6
  90.0 0.5 fusion.50
  90.6 0.5 fusion.51
  91.1 0.9 convolution_add_fusion.2
  92.1 0.1 convert_reduce_fusion.3
  92.2 0.3 compare_and_fusion.3
  92.5 1.1 constant_dynamic-slice_fusion.6
  93.6 0.5 fusion.50
  94.1 0.5 fusion.51
  94.7 0.9 convolution_add_fusion.2
  95.7 0.1 convert_reduce_fusion.3
  95.8 0.3 compare_and_fusion.3
  96.0 1.1 constant_dynamic-slice_fusion.6
  97.1 0.5 fusion.50
  97.7 0.5 fusion.51
  98.2 0.9 convolution_add_fusion.2
  99.2 0.1 convert_reduce_fusion.3
  99.3 0.3 compare_and_fusion.3
  99.6 1.1 constant_dynamic-slice_fusion.6
  100.7 0.5 fusion.50
  101.2 0.5 fusion.51
  101.8 0.9 convolution_add_fusion.2
  102.7 0.2 fusion.24
  103.0 0.2 copy.40
  103.2 0.2 convert_element_type.47
  103.4 0.6 gather_fusion
  103.9 4.6 %convolution_convert_fusion.1 = bf16[4,4096]{1,0:T(4,128)(2,1)S(1)} fusion(bf16[1024,4096]{1,0:T(8,128)(2,1)} %param.23, bf16[4,1024]{1,0:T(4,128)(2,1)S(1)} %gather_fusion, pred[4]{0:T(512)(128)(4,1)S(1)} %compare_and_fusion.1), kind=kOutput, calls=%fused_computation.38 | convolution fusion | flops 33574912 | bytes 8429572 | tf_op jit(solution)/shard_map/dot_general | solution.py:126
  108.6 1.4 copy.48
  110.0 20.1 %reduce-scatter.5.cloned.1.call-done = bf16[2048,4]{1,0:T(8,128)(2,1)} async-done(((bf16[4096,4]{1,0:T(8,128)(2,1)}), bf16[2048,4]{1,0:T(8,128)(2,1)}) %reduce-scatter.5.cloned.1.call-update) | async-done | bytes 16400
  130.1 1.2 copy.49
  131.4 0.1 multiply_reduce_fusion
  131.5 4.9 %psum.7 = f32[4]{0:T(128)S(1)} all-reduce(f32[4]{0:T(128)S(1)} %multiply_reduce_fusion), channel_id=1, replica_groups=mesh['ctx'=16,'head'=2] {'head'}, use_global_device_ids=true, to_apply=%region_9.10 | all-reduce | flops 4 | bytes 32 | tf_op jit(solution)/shard_map/psum | solution.py:131
  136.5 0.1 fusion.25
  136.6 22.0 %all-gather.3 = bf16[16,4,2048]{2,1,0:T(4,128)(2,1)S(1)} all-gather(bf16[1,4,2048]{2,1,0:T(4,128)(2,1)S(1)} %fusion.25), channel_id=1, replica_groups=mesh['ctx'=16,'head'=2] {'ctx'}, dimensions={0}, use_global_device_ids=true | all-gather | bytes 278528 | tf_op jit(solution)/shard_map/all_gather | solution.py:137
  158.7 15.7 %convolution_convert_fusion = bf16[64,8016]{1,0:T(8,128)(2,1)} fusion(bf16[64,2048]{1,0:T(8,128)(2,1)S(1)} %reshape.126, bf16[2048,8016]{0,1:T(8,128)(2,1)} %param.24), kind=kOutput, calls=%fused_computation.37 | convolution fusion | flops 2101859328 | bytes 34121728 | tf_op jit(solution)/shard_map/dot_general | solution.py:136
  174.4 0.6 dynamic-slice
  175.7 34.9 %all-reduce.7.cloned.1.call-done = bf16[64,8016]{1,0:T(8,128)(2,1)} async-done(((bf16[64,8016]{1,0:T(8,128)(2,1)}), bf16[64,8016]{1,0:T(8,128)(2,1)}) %all-reduce.7.cloned.1.call-update) | async-done | bytes 1026064
  210.6 1.4 dynamic-slice_reduce_fusion
  212.0 0.1 convert_dynamic-update-slice_fusion
  212.1 1.6 fusion.23
  213.7 0.3 dynamic-update-slice.2
  214.0 0.3 dynamic-update-slice.1
  214.3 39.5 %all-reduce.4 = (f32[2048]{0:T(1024)S(1)}, f32[2048]{0:T(1024)S(1)}, f32[2048]{0:T(1024)S(1)}) all-reduce(f32[2048]{0:T(1024)S(1)} %convert_dynamic-update-slice_fusion, f32[2048]{0:T(1024)S(1)} %dynamic-update-slice.1, f32[2048]{0:T(1024)S(1)} %dynamic-update-slice.2), channel_id=2, replica_groups=mesh['ctx'=16,'head'=2] {'ctx','head'}, use_global_device_ids=true, to_apply=%add | all-reduce | flops 6144 | bytes 49152
  253.8 0.1 slice.35
  253.8 0.1 slice.36
  253.9 0.1 slice.37
  254.0 0.1 reshape.116
  254.1 0.1 reshape.117
  254.1 0.1 reshape.118
  254.2 1.4 while.32
  255.6 0.5 minimum_negate_fusion
  (92 shorter events, 1.5 us)
Async XLA Ops:
  7.2 42.9 %all-gather.7.cloned.1.call-start = ((), (), s32[]{:S(2)}) async-start(), calls=%async_computation.1 | async-start | bytes 1114112 | tf_op jit(solution)/shard_map/all_gather | solution.py:114
  8.8 79.7 %all-gather.9.cloned.1.call-start = ((), (), s32[]{:S(2)}) async-start(), calls=%async_computation.2 | async-start | bytes 1114112 | tf_op jit(solution)/shard_map/all_gather | solution.py:115
  10.4 119.7 %reduce-scatter.5.cloned.1.call-start = ((), (), s32[]{:S(2)}) async-start(), calls=%async_computation.3 | async-start | bytes 1572864
  103.3 5.2 %copy-start = (bf16[128,1024]{1,0:T(8,128)(2,1)}, bf16[128,1024]{1,0:T(8,128)(2,1)S(1)}, u32[]{:S(2)}) copy-start(bf16[128,1024]{1,0:T(8,128)(2,1)S(1)} %convert_element_type.47) | copy-start | bytes 786436
  108.5 22.8 %copy-start.1 = (bf16[4,2048]{1,0:T(4,128)(2,1)S(1)}, bf16[4,2048]{1,0:T(4,128)(2,1)}, u32[]{:S(2)}) copy-start(bf16[4,2048]{1,0:T(4,128)(2,1)} %param.21) | copy-start | bytes 49156
  108.5 27.9 %copy-start.2 = (f32[2048]{0:T(1024)S(1)}, f32[2048]{0:T(1024)}, u32[]{:S(2)}) copy-start(f32[2048]{0:T(1024)} %param.22) | copy-start | bytes 24580
  110.0 100.6 %all-reduce.7.cloned.1.call-start = ((), (), s32[]{:S(2)}) async-start(), calls=%async_computation.4 | async-start | bytes 2064384
  158.7 15.8 %copy-start.6 = (u32[32]{0:T(128)S(1)}, u32[32]{0:T(128)}, u32[]{:S(2)}) copy-start(u32[32]{0:T(128)} %constant.134) | copy-start | bytes 388
  158.7 17.0 %copy-start.5 = (s32[64]{0:T(128)S(1)}, s32[64]{0:T(128)}, u32[]{:S(2)}) copy-start(s32[64]{0:T(128)} %param.25) | copy-start | bytes 772
  174.4 81.2 %copy-start.3 = (f32[64]{0:T(128)S(1)}, f32[64]{0:T(128)}, u32[]{:S(2)}) copy-start(f32[64]{0:T(128)} %param.27) | copy-start | bytes 772
  174.4 81.2 %copy-start.4 = (f32[64]{0:T(128)S(1)}, f32[64]{0:T(128)}, u32[]{:S(2)}) copy-start(f32[64]{0:T(128)} %param.26) | copy-start | bytes 772
Sparse Core Ops, SparseCore 0:
  10.7 39.3 all-gather.6
  52.3 36.2 all-gather.8
  110.1 19.9 reduce-scatter.4
  174.5 36.0 all-reduce.6
where the time goes:
time: 263 us
  waiting for transfers between devices  130 us (49%)
  blocking collectives  66.5 us (25%)
  matrix products  26.3 us (10%)
  between operations  14.6 us (6%)
  local copies, waits for them, and re-layouts  14 us (5%)
  other arithmetic  10.9 us (4%)
    unnamed x6, waiting for transfers between devices  55.1 us
    unnamed x1, blocking collectives  39.5 us
    all_gather x1, waiting for transfers between devices, per_device(): lax.all_gather(value_matrix, 'ctx', axis=0, tiled=True)  38.4 us
    all_gather x1, waiting for transfers between devices, per_device(): lax.all_gather(rotated_keys, 'ctx', axis=0, tiled=True)  36 us
    all_gather x1, blocking collectives, per_device(): lax.all_gather(normed, 'ctx', axis=0, tiled=True)  22 us
    dot_general x1, matrix products, per_device(): jnp.dot(lax.all_gather(normed, 'ctx', axis=0, tiled=True), lm_weight, pre...  15.7 us
    unnamed x27, local copies, waits for them, and re-layouts  8.32 us
  transfers between devices with their start and end apart: 4, of which 4 were waited for; matrix products, arithmetic and copies ran while one was open for 2% of the time, Pallas kernels for 0%

commit v1 on v0

v1 whole, which is shorter than its diff:
```python
import functools

import jax
import jax.numpy as jnp
from jax import lax
from jax.experimental import pallas as pl
from jax.experimental.pallas import tpu as pltpu
from jax.sharding import PartitionSpec as P

HEAD_SIZE = 128
MESH = pl.DeviceIdType.MESH
MASKED = -1e30
QUAD = 4


def kernel(
    n,
    heads,
    tile,
    split,
    doc_ref,
    scored_ref,
    q_hbm,
    k_hbm,
    v_hbm,
    res_hbm,
    gain_hbm,
    wo_hbm,
    lm_hbm,
    ids_hbm,
    att_out,
    logp_ref,
    q_in,
    kv,
    qs,
    acc,
    top,
    tot,
    att,
    res,
    gain,
    wo,
    lm,
    ids,
    part,
    psend,
    precv,
    hid,
    u,
    rows32,
    rows16,
    lsend,
    lrecv,
    own,
    stats,
    in_sem,
    lm_sem,
    a_send,
    a_recv,
    x_send,
    x_recv,
    c_send,
    c_recv,
    y_send,
    y_recv,
    u_send,
    u_recv,
    d_send,
    d_recv,
    l_send,
    l_recv,
    s_send,
    s_recv,
):
    me = lax.axis_index("ctx")
    h = lax.axis_index("head")
    groups = n // QUAD
    g = me // QUAD
    r = me % QUAD
    rx = (r + 2) % QUAD
    rc = r + 1 - 2 * (r % 2)
    rd = (rc + 2) % QUAD
    base = me - r
    x_peer = base + rx
    c_peer = base + rc
    y_peer = 1 - h
    tok = q_in.shape[0]
    kv_heads = k_hbm.shape[1] // HEAD_SIZE
    per = q_in.shape[1] // k_hbm.shape[1]
    resp = u.shape[1]
    rows = n * resp
    half = res.shape[2]
    vocab = lm.shape[0]

    def local(src, dst, k):
        copy = pltpu.make_async_copy(src, dst, in_sem.at[k])
        copy.start()
        return copy

    def remote(src, dst, ss, rs, where):
        return pltpu.make_async_remote_copy(
            src_ref=src, dst_ref=dst, send_sem=ss, recv_sem=rs, device_id=where, device_id_type=MESH
        )

    def at(c):
        return {"ctx": c, "head": h}

    across = {"ctx": me, "head": y_peer}

    in_k = local(k_hbm, kv.at[me, 0], 0)
    in_v = local(v_hbm, kv.at[me, 1], 1)
    in_q = local(q_hbm, q_in, 2)
    in_res = local(res_hbm, res.at[h], 3)

    barrier = pltpu.get_barrier_semaphore()

    def greet(c, carry):
        for k in range(heads):
            @pl.when(jnp.logical_or(c != me, h != k))
            def _():
                pl.semaphore_signal(
                    barrier, inc=1, device_id={"ctx": c, "head": k}, device_id_type=MESH
                )
        return carry

    lax.fori_loop(0, n, greet, 0)
    in_gain = local(gain_hbm, gain, 4)
    in_ids = local(ids_hbm, ids, 5)
    in_wo = local(wo_hbm, wo, 8)
    in_k.wait()
    in_v.wait()
    in_res.wait()
    pl.semaphore_wait(barrier, n * heads - 1)

    later = g + 1 < groups

    def z_copy(src, p):
        piece = kv.at[src * QUAD + r, p]
        return remote(piece, piece, a_send.at[p, src], a_recv.at[p, src], at(me + QUAD))

    def x_copy(src, off, p):
        piece = kv.at[src * QUAD + off, p]
        return remote(piece, piece, x_send.at[p, src], x_recv.at[p, src], at(x_peer))

    def c_copy(src, off, kind, p):
        piece = kv.at[src * QUAD + off, p]
        return remote(piece, piece, c_send.at[kind, p, src], c_recv.at[kind, p, src], at(c_peer))

    def spread(src, p):
        @pl.when(later)
        def _():
            z_copy(src, p).start()

        x_copy(src, r, p).start()
        c_copy(src, r, 0, p).start()

    for p in range(2):
        spread(g, p)
    res_copy = remote(res.at[h], res.at[h], y_send.at[0], y_recv.at[0], across)
    res_copy.start()

    lm_rows = pl.cdiv(pl.cdiv(vocab, 8), 16) * 16
    lm_copies = []
    for k in range(pl.cdiv(vocab, lm_rows)):
        s = pl.ds(k * lm_rows, min(lm_rows, vocab - k * lm_rows))
        copy = pltpu.make_async_copy(lm_hbm.at[s], lm.at[s], lm_sem.at[k])
        copy.start()
        lm_copies.append(copy)

    in_q.wait()
    for hh in range(kv_heads * per):
        qs[hh // per, pl.ds((hh % per) * tok, tok), :] = q_in[:, hh * HEAD_SIZE : (hh + 1) * HEAD_SIZE]

    ends = [doc_ref[0]]
    for k in range(1, doc_ref.shape[0]):
        ends.append(ends[-1] + doc_ref[k])
    qpos = me * tok + lax.broadcasted_iota(jnp.int32, (per, tok, 1), 1).reshape(per * tok, 1)
    first = jnp.zeros_like(qpos)
    for e in ends:
        first = jnp.where(qpos >= e, e, first)

    width = QUAD * tok

    def attend(src, fresh):
        kpos = src * width + lax.broadcasted_iota(jnp.int32, (1, width), 1)
        allowed = jnp.logical_and(kpos <= qpos, kpos >= first)
        for kh in range(kv_heads):
            lanes = slice(kh * HEAD_SIZE, (kh + 1) * HEAD_SIZE)
            keys = kv[pl.ds(src * QUAD, QUAD), 0, :, lanes].reshape(width, HEAD_SIZE)
            vals = kv[pl.ds(src * QUAD, QUAD), 1, :, lanes].reshape(width, HEAD_SIZE)
            s = lax.dot_general(
                qs[kh], keys, (((1,), (1,)), ((), ())), preferred_element_type=jnp.float32
            ) * HEAD_SIZE ** (-0.5)
            s = jnp.where(allowed, s, MASKED)
            peak = jnp.max(s, axis=1, keepdims=True)
            if fresh:
                new = peak
            else:
                new = jnp.maximum(top[kh], peak)
            w = jnp.exp(s - new)
            total = jnp.sum(w, axis=1, keepdims=True)
            upd = jnp.dot(w.astype(jnp.bfloat16), vals, preferred_element_type=jnp.float32)
            if fresh:
                acc[kh] = upd
                tot[kh] = total
            else:
                fix = jnp.exp(top[kh] - new)
                acc[kh] = acc[kh] * fix + upd
                tot[kh] = tot[kh] * fix + total
            top[kh] = new

    def settle(src):
        for p in range(2):
            x_copy(src, rx, p).wait_recv()
            c_copy(src, rx, 1, p).start()
        for p in range(2):
            c_copy(src, rc, 0, p).wait_recv()
            c_copy(src, rd, 1, p).wait_recv()

    def pull(src):
        for p in range(2):
            z_copy(src, p).wait_recv()
            spread(src, p)

    @pl.when(g > 0)
    def _():
        pull(g - 1)

    settle(g)
    attend(g, True)

    def step(d, carry):
        @pl.when(d < g)
        def _():
            pull(g - d - 1)

        settle(g - d)
        attend(g - d, False)
        return carry

    lax.fori_loop(1, g + 1, step, 0)

    for kh in range(kv_heads):
        out = (acc[kh] / tot[kh]).astype(jnp.bfloat16)
        for j in range(per):
            hh = kh * per + j
            att[:, hh * HEAD_SIZE : (hh + 1) * HEAD_SIZE] = out[j * tok : (j + 1) * tok]
    att_copy = local(att, att_out, 9)

    pick = lax.broadcasted_iota(jnp.int32, (8, tok), 1)
    line = lax.broadcasted_iota(jnp.int32, (8, tok), 0)
    wanted = jnp.full((8, tok), -1, jnp.int32)
    for k in range(resp):
        wanted = jnp.where(line == k, scored_ref[k], wanted)
    onehot = jnp.where(pick == wanted, 1.0, 0.0).astype(jnp.bfloat16)
    chosen = jnp.dot(onehot, att[...], preferred_element_type=jnp.float32).astype(jnp.bfloat16)
    in_wo.wait()
    cols = 2048

    def project(t, carry):
        s = pl.ds(pl.multiple_of(t * cols, cols), cols)
        piece = jnp.dot(chosen, wo[:, s], preferred_element_type=jnp.float32)[:resp]
        part[:, s] = piece
        psend[:, s] = piece.astype(jnp.bfloat16)
        return carry

    lax.fori_loop(0, wo.shape[1] // cols, project, 0)
    p_copy = remote(psend, precv, y_send.at[1], y_recv.at[1], across)
    p_copy.start()
    in_gain.wait()
    in_ids.wait()
    ids_col = jnp.transpose(
        jnp.broadcast_to(ids[...].astype(jnp.float32), (128, rows))
    )[:, 0:1].astype(jnp.int32)
    res_copy.wait()
    p_copy.wait()
    squares = jnp.zeros((resp, 1), jnp.float32)
    for k in range(heads):
        s = slice(k * half, (k + 1) * half)
        value = res[k].astype(jnp.float32) + (part[:, s] + precv[:, s].astype(jnp.float32))
        hid[k] = value
        squares = squares + jnp.sum(value * value, axis=1, keepdims=True)
    normed = hid[h] * lax.rsqrt(squares / (half * heads) + 1e-05) * gain[...]
    u[me] = normed.astype(jnp.bfloat16)

    core = me % 2
    mate = me + 1 - 2 * core
    chips = n // 2
    chip = me // 2

    def u_copy(c, dst):
        b = c * 2 + core
        return remote(u.at[b], u.at[b], u_send.at[dst], u_recv.at[c], at(dst * 2 + core))

    def d_copy(c, side):
        b = c * 2 + side
        return remote(u.at[b], u.at[b], d_send.at[c], d_recv.at[c], at(mate))

    def u_start(k, carry):
        u_copy(chip, (chip + k) % chips).start()
        return carry

    lax.fori_loop(1, chips, u_start, 0)
    d_copy(chip, core).start()

    def u_pass(k, carry):
        c = (chip + k) % chips
        u_copy(c, 0).wait_recv()
        d_copy(c, core).start()
        return carry

    lax.fori_loop(1, chips, u_pass, 0)

    def u_take(c, carry):
        d_copy(c, 1 - core).wait_recv()
        rows32[c, 0:resp, :] = u[2 * c].astype(jnp.float32)
        rows32[c, resp : 2 * resp, :] = u[2 * c + 1].astype(jnp.float32)
        return carry

    lax.fori_loop(0, chips, u_take, 0)
    rows16[...] = rows32[...].reshape(rows, half).astype(jnp.bfloat16)
    for copy in lm_copies:
        copy.wait()

    full = (vocab - split) // tile
    tails = (split - full * tile, vocab - split - full * tile)

    def l_copy(t):
        return remote(lsend.at[t], lrecv.at[t], l_send.at[t], l_recv.at[t], across)

    def columns(side, t):
        return pl.ds(pl.multiple_of(side * split + t * tile, 128), tile)

    def dot_columns(s):
        return lax.dot_general(
            rows16[...], lm[s, :], (((1,), (1,)), ((), ())), preferred_element_type=jnp.float32
        )

    def far(t, carry):
        lsend[t] = dot_columns(columns(y_peer, t)).astype(jnp.bfloat16)
        l_copy(t).start()
        return carry

    lax.fori_loop(0, full, far, 0)
    for k in range(2):
        if tails[k]:
            @pl.when(y_peer == k)
            def _():
                start = k * split + full * tile
                lsend[full, :, 0 : tails[k]] = dot_columns(slice(start, start + tails[k])).astype(jnp.bfloat16)
    if max(tails):
        l_copy(full).start()

    def near(t, carry):
        own[t] = dot_columns(columns(h, t))
        return carry

    lax.fori_loop(0, full, near, 0)
    for k in range(2):
        if tails[k]:
            @pl.when(h == k)
            def _():
                start = k * split + full * tile
                own[full, :, 0 : tails[k]] = dot_columns(slice(start, start + tails[k]))

    first_id = me * vocab + h * split
    last_tail = jnp.where(h == 0, tails[0], tails[1])

    def fold(t, state, limit):
        peak, total, target = state
        l_copy(t).wait_recv()
        z = own[t] + lrecv[t].astype(jnp.float32)
        lane = lax.broadcasted_iota(jnp.int32, (rows, tile), 1)
        if limit is not None:
            z = jnp.where(lane < limit, z, MASKED)
        hit = lane == ids_col - (first_id + t * tile)
        if limit is not None:
            hit = jnp.logical_and(hit, lane < limit)
        else:
            pass
        target = target + jnp.sum(jnp.where(hit, z, 0.0), axis=1, keepdims=True)
        new = jnp.maximum(peak, jnp.max(z, axis=1, keepdims=True))
        total = total * jnp.exp(peak - new) + jnp.sum(jnp.exp(z - new), axis=1, keepdims=True)
        return new, total, target

    state = (
        jnp.full((rows, 1), MASKED, jnp.float32),
        jnp.zeros((rows, 1), jnp.float32),
        jnp.zeros((rows, 1), jnp.float32),
    )
    state = lax.fori_loop(0, full, lambda t, c: fold(t, c, None), state)
    if max(tails):
        state = fold(full, state, last_tail)
    peak, total, target = state

    lane = lax.broadcasted_iota(jnp.int32, (rows, 128), 1)
    block = jnp.where(lane == 0, peak, jnp.where(lane == 1, total, jnp.where(lane == 2, target, 0.0)))
    flat = me * heads + h
    stats[flat] = jnp.transpose(block)[0:8]

    def s_copy(src, dst):
        return remote(
            stats.at[src],
            stats.at[src],
            s_send.at[dst],
            s_recv.at[src],
            {"ctx": dst // heads, "head": dst % heads},
        )

    everyone = n * heads

    def s_start(k, carry):
        s_copy(flat, (flat + k) % everyone).start()
        return carry

    lax.fori_loop(1, everyone, s_start, 0)

    def g_end(src, carry):
        for p in range(2):
            @pl.when(later)
            def _():
                z_copy(src, p).wait_send()

            x_copy(src, r, p).wait_send()
            c_copy(src, r, 0, p).wait_send()
            c_copy(src, rx, 1, p).wait_send()
        return carry

    lax.fori_loop(0, g + 1, g_end, 0)

    def u_end(k, carry):
        u_copy(chip, (chip + k) % chips).wait_send()
        return carry

    lax.fori_loop(1, chips, u_end, 0)

    def d_end(c, carry):
        d_copy(c, core).wait_send()
        return carry

    lax.fori_loop(0, chips, d_end, 0)

    def l_end(t, carry):
        l_copy(t).wait_send()
        return carry

    lax.fori_loop(0, full + (1 if max(tails) else 0), l_end, 0)
    att_copy.wait()

    def s_wait(k, carry):
        s_copy((flat + k) % everyone, 0).wait_recv()
        return carry

    lax.fori_loop(1, everyone, s_wait, 0)
    every = stats[...]
    peaks, totals, targets = every[:, 0:1, :], every[:, 1:2, :], every[:, 2:3, :]
    best = jnp.max(peaks, axis=0)
    total = jnp.sum(totals * jnp.exp(peaks - best[None]), axis=0)
    lead = jnp.sum(targets, axis=0) - best
    logp_ref[0:1, :] = lead
    logp_ref[1:2, :] = total

    def s_end(k, carry):
        s_copy(flat, (flat + k) % everyone).wait_send()
        return carry

    lax.fori_loop(1, everyone, s_end, 0)


def per_device(
    n,
    heads,
    queries,
    rotated_keys,
    value_matrix,
    doc_lengths,
    scored,
    residual,
    norm_gain,
    out_weight,
    lm_weight,
    token_ids,
    old_logp,
    advantage,
):
    tok, feats = queries.shape
    kv_feats = rotated_keys.shape[1]
    kv_heads = kv_feats // HEAD_SIZE
    per = feats // kv_feats
    resp = scored.shape[0]
    rows = n * resp
    half = residual.shape[1]
    width = half * heads
    depth, vocab = lm_weight.shape
    tile = 512
    split = pl.cdiv(pl.cdiv(vocab, 2), tile) * tile
    tiles = pl.cdiv(split, tile)
    groups = n // QUAD
    chips = n // 2
    bf16, f32 = jnp.bfloat16, jnp.float32
    vm, dma = pltpu.VMEM, pltpu.SemaphoreType.DMA
    hbm = pl.BlockSpec(memory_space=pl.ANY)
    smem = pl.BlockSpec(memory_space=pltpu.SMEM)
    vmem = pl.BlockSpec(memory_space=pltpu.VMEM)
    attended, pair = pl.pallas_call(
        functools.partial(kernel, n, heads, tile, split),
        out_shape=(
            jax.ShapeDtypeStruct((tok, feats), bf16),
            jax.ShapeDtypeStruct((2, rows), f32),
        ),
        in_specs=[smem, smem] + [hbm] * 8,
        out_specs=(hbm, vmem),
        scratch_shapes=[
            vm((tok, feats), bf16),
            vm((n, 2, tok, kv_feats), bf16),
            vm((kv_heads, per * tok, HEAD_SIZE), bf16),
            vm((kv_heads, per * tok, HEAD_SIZE), f32),
            vm((kv_heads, per * tok, 1), f32),
            vm((kv_heads, per * tok, 1), f32),
            vm((tok, feats), bf16),
            vm((heads, resp, half), bf16),
            vm((1, half), f32),
            vm(out_weight.shape, bf16),
            vm((vocab, depth), bf16),
            vm((1, rows), jnp.int32),
            vm((resp, width), f32),
            vm((resp, width), bf16),
            vm((resp, width), bf16),
            vm((heads, resp, half), f32),
            vm((n, resp, half), bf16),
            vm((chips, 2 * resp, half), f32),
            vm((rows, half), bf16),
            vm((tiles, rows, tile), bf16),
            vm((tiles, rows, tile), bf16),
            vm((tiles, rows, tile), f32),
            vm((n * heads, 8, rows), f32),
            dma((10,)),
            dma((8,)),
            dma((2, groups)),
            dma((2, groups)),
            dma((2, groups)),
            dma((2, groups)),
            dma((2, 2, groups)),
            dma((2, 2, groups)),
            dma((2,)),
            dma((2,)),
            dma((chips,)),
            dma((chips,)),
            dma((chips,)),
            dma((chips,)),
            dma((tiles,)),
            dma((tiles,)),
            dma((n * heads,)),
            dma((n * heads,)),
        ],
        compiler_params=pltpu.CompilerParams(
            collective_id=0, has_side_effects=True, vmem_limit_bytes=67043328 - (1 << 20)
        ),
    )(
        doc_lengths,
        scored,
        queries,
        rotated_keys,
        value_matrix,
        residual,
        norm_gain.reshape(1, half),
        out_weight,
        lm_weight.T,
        token_ids.reshape(1, rows),
    )
    log_probs = pair[0] - jnp.log(pair[1])
    ratio = jnp.exp(jnp.clip(log_probs - old_logp, -4.0, 4.0))
    token_loss = -jnp.minimum(ratio * advantage, jnp.clip(ratio, 0.8, 1.2) * advantage)
    return attended, log_probs, token_loss


def solution(mesh):
    return jax.shard_map(
        functools.partial(per_device, mesh.shape["ctx"], mesh.shape["head"]),
        mesh=mesh,
        in_specs=(
            P("ctx", "head"),
            P("ctx", "head"),
            P("ctx", "head"),
            P(),
            P("ctx"),
            P("ctx", "head"),
            P("head"),
            P("head", None),
            P("head", "ctx"),
            P(),
            P(),
            P(),
        ),
        out_specs=(P("ctx", "head"), P(), P()),
        check_vma=False,
    )
```

time: 263 us -> 61.6 us (0.23)
  waiting for transfers between devices: 130 us -> 0 us
  blocking collectives: 66.5 us -> 0 us
  Pallas kernels: 0 us -> 57.8 us
  matrix products: 26.3 us -> 0 us
  between operations: 14.6 us -> 0.68 us
  local copies, waits for them, and re-layouts: 14 us -> 1.68 us
  other arithmetic: 10.9 us -> 1.29 us
    all_gather x2 -> x0, waiting for transfers between devices: 74.4 us -> none  [the longest x1 38.4 us: per_device(): lax.all_gather(value_matrix, 'ctx', axis=0, tiled=True)]
    pallas_call x0 -> x1, Pallas kernels: none -> 57.8 us  [per_device(): pl.pallas_call(functools.partial(kernel, n, heads, tile, split), out_shap...]
    unnamed x6 -> x0, waiting for transfers between devices: 55.1 us -> none
    unnamed x1 -> x0, blocking collectives: 39.5 us -> none
    dot_general x10 -> x0, matrix products: 26.3 us -> none  [the longest x1 15.7 us: per_device(): jnp.dot(lax.all_gather(normed, 'ctx', axis=0, tiled=True), lm_weight, pre...]
    all_gather x1 -> x0, blocking collectives: 22 us -> none  [per_device(): lax.all_gather(normed, 'ctx', axis=0, tiled=True)]
    unnamed x27 -> x5, local copies, waits for them, and re-layouts: 8.32 us -> 1.68 us
    psum x1 -> x0, blocking collectives: 4.93 us -> none  [per_device(): squares = lax.psum(jnp.sum(hidden * hidden, axis=1), 'head')]
  transfers between devices with their start and end apart: 4 -> 0, of which waited for: 4 -> 0; matrix products, arithmetic and copies ran while one was open for 2% -> 0% of each run, Pallas kernels for 0% -> 0%
where the time goes in v1:
time: 61.6 us; the launch traced here: 61.4 us
  Pallas kernels  57.8 us (94%)
  local copies, waits for them, and re-layouts  1.68 us (3%)
  other arithmetic  1.29 us (2%)
  between operations  0.68 us (1%)
    pallas_call x1, Pallas kernels, per_device(): pl.pallas_call(functools.partial(kernel, n, heads, tile, split), out_shap...  57.8 us
    unnamed x5, local copies, waits for them, and re-layouts  1.68 us
    neg x1, other arithmetic, per_device(): -jnp.minimum(ratio * advantage, jnp.clip(ratio, 0.8, 1.2) * advantage)  1.29 us

profile of v1, /device:TPU:0, one launch (start us, length us, event | category | flops | bytes accessed | tf_op | source)
XLA Modules:
  0.0 61.4 jit_solution(17020170583710918348)
XLA Ops:
  0.6 0.0 copy-start
  0.6 0.0 copy-start.1
  0.7 57.8 %shard_map.139 = (bf16[128,1024]{1,0:T(8,128)(2,1)}, f32[2,64]{1,0:T(2,128)}) custom-call(s32[8]{0:T(128)} %doc_ref.1, s32[4]{0:T(128)} %scored_ref.1, bf16[128,1024]{1,0:T(8,128)(2,1)} %q_hbm.1, bf16[128,256]{1,0:T(8,128)(2,1)} %k_hbm.1, bf16[128,256]{1,0:T(8,128)(2,1)} %v_hbm.1, bf16[4,2048]{1,0:T(4,128)(2,1)} %res_hbm.1, f32[1,2048]{1,0:T(1,128)} %bitcast.7, ...), custom_call_target="tpu_custom_call" | custom-call | tf_op jit(solution)/shard_map/pallas_call | solution.py:505
  58.4 0.0 copy-done
  58.5 0.0 copy-done.1
  58.5 1.3 %minimum_negate_fusion = (f32[64]{0:T(128)}, f32[64]{0:T(128)}) fusion(f32[64]{0:T(128)S(1)} %copy-done, f32[64]{0:T(128)S(1)} %copy-done.1, f32[2,64]{1,0:T(2,128)} %get-tuple-element.6), kind=kLoop, calls=%fused_computation | loop fusion | flops 512 | bytes 1536 | tf_op jit(solution)/shard_map/neg | solution.py:573
  59.8 1.7 %copy.16 = bf16[128,1024]{1,0:T(8,128)(2,1)} copy(bf16[128,1024]{1,0:T(8,128)(2,1)} %get-tuple-element.12) | data formatting | bytes 524288
Async XLA Ops:
  0.6 57.8 %copy-start = (f32[64]{0:T(128)S(1)}, f32[64]{0:T(128)}, u32[]{:S(2)}) copy-start(f32[64]{0:T(128)} %param.23) | copy-start | bytes 772
  0.6 57.8 %copy-start.1 = (f32[64]{0:T(128)S(1)}, f32[64]{0:T(128)}, u32[]{:S(2)}) copy-start(f32[64]{0:T(128)} %param.22) | copy-start | bytes 772
